TPU v7x, 32 devices: a whole 2x2x4 slice. The times are simulated.
32 devices in a mesh: row: 4 (over z), col: 8 (over y, x, core).
Axes of the slice: x: 2, y: 2, z: 4, core: 2. Of those that a mesh axis runs over, the one named last changes fastest.
Arguments:
- gram: bfloat16 [2, 4, 384, 1, 8, 384], P(None, 'row', None, None, 'col'), may hold values from -1 to 20, as said below
Outputs:
- swept: float32 [2, 4, 384, 1, 8, 384], P(None, 'row', None, None, 'col')
Inputs may be any that keep to these rules, and one draw needn't show every extreme that they name: gram is symmetric and positive definite.
All inputs are finite; a program needn't handle non-finite values.
Results may differ from a plain program's by a relative error of at most 0.0003.
Values sent between devices are 32-bit elements; how exact they have to be, the bound alone decides.
No kernel may reach another device: no remote copies, remote signals or barrier semaphores. Data moves between devices by JAX's collectives and lax.ppermute only.
A program may use at most 64 MiB of HBM per device.

v0:
```python
import jax
import jax.numpy as jnp
from jax import lax
from jax.experimental import pallas as pl
from jax.experimental.pallas import tpu as pltpu
from jax.sharding import PartitionSpec as P


LEAF = 16
LANES = 128


def split(value):
    high = value.astype(jnp.bfloat16).astype(jnp.float32)
    rest = value - high
    middle = rest.astype(jnp.bfloat16).astype(jnp.float32)
    return high, middle, (rest - middle).astype(jnp.bfloat16).astype(jnp.float32)


def invert(ref, left_ref):
    order = ref.shape[0]
    blocks = order // LANES
    groups = LANES // LEAF
    rows_leaf = lax.broadcasted_iota(jnp.int32, (LEAF, LANES), 0)
    rows_wide = lax.broadcasted_iota(jnp.int32, (LEAF, order), 0)
    lanes_wide = lax.broadcasted_iota(jnp.int32, (LEAF, order), 1)
    lanes_left = lax.broadcasted_iota(jnp.int32, (order, LANES), 1)
    nothing = jnp.zeros((LEAF, order), jnp.bfloat16)

    def block(number, _):
        base = pl.multiple_of(number * LANES, LANES)
        lanes = pl.ds(base, LANES)
        wide = ref[pl.ds(base, LEAF), :]
        tile = ref[pl.ds(base, LEAF), lanes]
        for group in range(groups):
            lower = group * LEAF
            rows = pl.ds(pl.multiple_of(base + lower, LEAF), LEAF)
            left = ref[:, lanes]
            inside = (lanes_left >= lower) & (lanes_left < lower + LEAF)
            high, middle, low = split(jnp.where(inside, left, 0.0))
            twice = high + pltpu.roll(middle, LEAF, 1)
            packed = twice + pltpu.roll(twice, 2 * LEAF, 1)
            packed = packed + pltpu.roll(high, 4 * LEAF, 1) + pltpu.roll(low, 5 * LEAF, 1)
            left_ref[...] = packed.astype(jnp.bfloat16)
            ref[:, lanes] = jnp.where(inside, 0.0, left)
            columns = [
                jnp.broadcast_to(tile[:, lower + k : lower + k + 1], (LEAF, LANES))
                for k in range(LEAF)
            ]
            here = lanes_wide - (base + lower)
            unit = jnp.where(here == rows_wide, 1.0, 0.0)
            wide = jnp.where((here >= 0) & (here < LEAF), unit, wide)
            parts = [wide[:, part * LANES : (part + 1) * LANES] for part in range(blocks)]
            for k in range(LEAF):
                pivot = columns[k][k : k + 1, :]
                inverted = 1.0 / pivot
                factor = jnp.where(rows_leaf == k, pivot - 1.0, columns[k])
                for later in range(k + 1, LEAF):
                    row = columns[later][k : k + 1, :] * inverted
                    columns[later] = columns[later] - factor * row
                parts = [part - factor * (part[k : k + 1, :] * inverted) for part in parts]
            done = jnp.concatenate(parts, axis=1)
            high, middle, low = [part.astype(jnp.bfloat16) for part in split(done)]
            pieces = [nothing] * groups
            for place, piece in enumerate((high, high, middle, middle, low, high)):
                pieces[(group + place) % groups] = piece
            right = jnp.concatenate(pieces, axis=0)
            if group < groups - 1:
                after = pl.ds(pl.multiple_of(base + lower + LEAF, LEAF), LEAF)
                change = jnp.dot(left_ref[after, :], right, preferred_element_type=jnp.float32)
                wide = ref[after, :] - change
                chosen = change[:, :LANES]
                for part in range(1, blocks):
                    chosen = jnp.where(
                        number == part, change[:, part * LANES : (part + 1) * LANES], chosen
                    )
                tile = ref[after, lanes] - chosen
            ref[...] = ref[...] - jnp.dot(
                left_ref[...], right, preferred_element_type=jnp.float32
            )
            ref[rows, :] = done
        return 0

    lax.fori_loop(0, blocks, block, 0)


def raw_dot(left, right, contract=(1, 0)):
    dims = (((contract[0],), (contract[1],)), ((), ()))
    return lax.dot_general(left, right, dims, preferred_element_type=jnp.float32)


def joined(terms, contract=(1, 0)):
    left = jnp.concatenate([term[0] for term in terms], axis=contract[0])
    right = jnp.concatenate([term[1] for term in terms], axis=contract[1])
    return raw_dot(left, right, contract)


def halves(value):
    return [part.astype(jnp.bfloat16) for part in split(value)]


def fetch(source, target, semaphore):
    copy = pltpu.make_async_copy(source, target, semaphore)
    copy.start()
    copy.wait()


def first_kernel(
    flags, own, sibling, lefts_out, ng_out, t_out, n_ref, a_ref, left_ref, semaphore, own_ref, more
):
    order = a_ref.shape[0]
    head = pl.ds(0, order)
    tail = pl.ds(order, own.shape[0] - order)

    fetch(own, own_ref, semaphore)

    @pl.when(flags[0] == 0)
    def _():
        fetch(own_ref, lefts_out, semaphore)

    @pl.when(flags[0] != 0)
    def _():
        @pl.when(flags[1] != 0)
        def _():
            n_ref[...] = own_ref[head, :]
            fetch(sibling, a_ref, semaphore)

        @pl.when(flags[1] == 0)
        def _():
            fetch(sibling, n_ref, semaphore)
            a_ref[...] = own_ref[head, :]

        invert(n_ref, left_ref)
        a10 = a_ref[...].astype(jnp.bfloat16)
        g = joined([(part, a10) for part in reversed(halves(n_ref[...]))])
        a_ref[...] = joined([(a10, part) for part in reversed(halves(g))], (0, 0))
        n_ref[...] = jnp.where(flags[1] != 0, g, n_ref[...])
        copies = [
            pltpu.make_async_copy(source, target, more.at[i])
            for i, (source, target) in enumerate(
                [
                    (n_ref, ng_out),
                    (a_ref, t_out),
                    (n_ref, lefts_out.at[head]),
                    (own_ref.at[tail], lefts_out.at[tail]),
                ]
            )
        ]
        for copy in copies:
            copy.start()
        for copy in copies:
            copy.wait()


def second_kernel(flags, t, a00, s_out, s_ref, a_ref, left_ref, semaphore):
    half = s_out.shape[0]

    @pl.when(flags[0] != 0)
    def _():
        fetch(t, a_ref, semaphore)
        fetch(a00, s_ref, semaphore)
        s_ref[...] = s_ref[...] - a_ref[...]
        invert(s_ref, left_ref)

        @pl.when(flags[1] != 0)
        def _():
            fetch(s_ref.at[pl.ds(half, half)], s_out, semaphore)

        @pl.when(flags[1] == 0)
        def _():
            fetch(s_ref.at[pl.ds(0, half)], s_out, semaphore)


def pivot_call(kernel, flags, left, right, outs, more=()):
    order = right.shape[0]
    anywhere = pl.BlockSpec(memory_space=pl.ANY)
    return pl.pallas_call(
        kernel,
        out_shape=[jax.ShapeDtypeStruct(shape, jnp.float32) for shape in outs],
        in_specs=[pl.BlockSpec(memory_space=pltpu.SMEM), anywhere, anywhere],
        out_specs=[anywhere] * len(outs),
        scratch_shapes=[
            pltpu.VMEM((order, order), jnp.float32),
            pltpu.VMEM((order, order), jnp.float32),
            pltpu.VMEM((order, LANES), jnp.bfloat16),
            pltpu.SemaphoreType.DMA,
            *more,
        ],
    )(flags, left, right)


def transfer(cases, semaphores, begin, place=0):
    for condition, copies in cases:
        @pl.when(condition)
        def _(copies=copies, place=place):
            for i, (source, target) in enumerate(copies):
                copy = pltpu.make_async_copy(source, target, semaphores.at[place + i])
                if begin:
                    copy.start()
                else:
                    copy.wait()

        place += len(copies)
    return place


def pack_kernel(flags, lefts, sibling, near, out, held, semaphores):
    order = out.shape[0] // 2
    at = pl.ds(pl.multiple_of(flags[1] * order, order), order)
    head, tail = pl.ds(0, order), pl.ds(order, order)
    far, odd = flags[0] != 0, flags[2] != 0
    cases = [
        (jnp.logical_not(far), [(near, held)]),
        (far & odd, [(sibling.at[at], held.at[head]), (lefts.at[at], held.at[tail])]),
        (
            far & jnp.logical_not(odd),
            [(lefts.at[at], held.at[head]), (sibling.at[at], held.at[tail])],
        ),
    ]
    transfer(cases, semaphores, True)
    transfer(cases, semaphores, False)
    fetch(held, out, semaphores.at[0])


def pack(flags, lefts, sibling, near):
    anywhere = pl.BlockSpec(memory_space=pl.ANY)
    return pl.pallas_call(
        pack_kernel,
        out_shape=jax.ShapeDtypeStruct(near.shape, jnp.float32),
        in_specs=[pl.BlockSpec(memory_space=pltpu.SMEM)] + [anywhere] * 3,
        out_specs=anywhere,
        scratch_shapes=[pltpu.VMEM(near.shape, jnp.float32), pltpu.SemaphoreType.DMA((5,))],
        name="pack",
    )(flags, lefts, sibling, near)


FIRST, SECOND, TOP, BOTTOM, NEAR, FAR, PACKED, LATER = range(8)


PRODUCTS = ((0, 2), (2, 0), (1, 1), (0, 1), (1, 0), (0, 0))


def finish_kernel(
    flags, mine, lefts, sibling, across, near, far, packed, ng, ng_sibling, s_mine, s_other, out,
    mine_ref, left0_ref, left1_ref, n_ref, g_ref, r_ref, s_ref, semaphores
):
    order = n_ref.shape[0]
    half = order // 2
    kind, odd, in_root, pivotal = flags[0], flags[1] != 0, flags[2] != 0, flags[3] != 0
    in_top = flags[4] != 0
    head, tail = pl.ds(0, order), pl.ds(order, order)
    upper, lower = s_ref.at[pl.ds(0, half)], s_ref.at[pl.ds(half, half)]
    even = jnp.logical_not(odd)
    elsewhere = jnp.logical_not(in_root)
    first = [
        (kind == TOP, [(mine.at[head], r_ref.at[head]), (across, r_ref.at[tail])]),
        (kind == BOTTOM, [(across, r_ref.at[head]), (mine.at[head], r_ref.at[tail])]),
        (kind == NEAR, [(near, r_ref)]),
        ((kind == FAR) | (kind == LATER), [(far, r_ref)]),
        (kind == PACKED, [(packed, r_ref)]),
        (elsewhere & even, [(ng, n_ref), (ng_sibling, g_ref)]),
        (elsewhere & odd, [(ng_sibling, n_ref), (ng, g_ref)]),
        (in_root & even, [(lefts.at[head], n_ref), (sibling.at[head], g_ref)]),
        (in_root & odd, [(sibling.at[head], n_ref), (lefts.at[head], g_ref)]),
        (even, [(s_mine, upper), (s_other, lower)]),
        (odd, [(s_other, upper), (s_mine, lower)]),
    ]
    second = [
        (even, [(lefts, left0_ref), (sibling, left1_ref)]),
        (odd, [(sibling, left0_ref), (lefts, left1_ref)]),
        (kind >= 0, [(mine, mine_ref)]),
    ]
    place = transfer(first, semaphores, True)
    transfer(second, semaphores, True, place)
    transfer(first, semaphores, False)

    @pl.when((kind == FAR) | (kind == PACKED))
    def _():
        r_ref[head, :] = r_ref[head, :].T
        r_ref[tail, :] = r_ref[tail, :].T

    @pl.when((kind == FIRST) | (kind == SECOND))
    def _():
        rows = lax.broadcasted_iota(jnp.int32, (order, order), 0)
        lanes = lax.broadcasted_iota(jnp.int32, (order, order), 1)
        unit = jnp.where(rows == lanes, 1.0, 0.0)
        r_ref[head, :] = jnp.where(kind == FIRST, unit, 0.0)
        r_ref[tail, :] = jnp.where(kind == FIRST, 0.0, unit)

    r1 = r_ref[tail, :].astype(jnp.bfloat16)
    g = halves(g_ref[...])
    n = halves(n_ref[...])
    s = halves(s_ref[...])
    y = halves(r_ref[head, :] - joined([(part, r1) for part in reversed(g)], (0, 0)))
    w0 = joined([(s[i], y[j]) for i, j in PRODUCTS])
    w = halves(w0)
    w1 = joined([(part, r1) for part in reversed(n)])
    w1 = w1 - joined([(g[i], w[j]) for i, j in PRODUCTS])
    v = halves(w1)
    transfer(second, semaphores, False, place)
    left0 = left0_ref[...].astype(jnp.bfloat16)
    left1 = left1_ref[...].astype(jnp.bfloat16)
    change = joined([(left0, w[i]) for i in (2, 1, 0)] + [(left1, v[i]) for i in (2, 1, 0)])
    mine_ref[...] = jnp.where(pivotal, 0.0, mine_ref[...]) - change

    @pl.when(in_top)
    def _():
        mine_ref[head, :] = w0

    @pl.when(in_root)
    def _():
        mine_ref[head, :] = w1

    count = order // LANES
    for part in range(count):
        where = pl.ds(part, mine_ref.shape[0], stride=count)
        out[where, :] = mine_ref[:, part * LANES : (part + 1) * LANES]


def finish(flags, *arrays):
    mine = arrays[0]
    order = mine.shape[1]
    anywhere = pl.BlockSpec(memory_space=pl.ANY)
    square, whole = pltpu.VMEM((order, order), jnp.float32), pltpu.VMEM(mine.shape, jnp.float32)
    linear = (mine.shape[0] * order // LANES, LANES)
    return pl.pallas_call(
        finish_kernel,
        out_shape=jax.ShapeDtypeStruct(linear, jnp.float32),
        in_specs=[pl.BlockSpec(memory_space=pltpu.SMEM)] + [anywhere] * len(arrays),
        out_specs=pl.BlockSpec(memory_space=pltpu.VMEM),
        scratch_shapes=[whole, whole, whole, square, square]
        + [pltpu.VMEM((2 * order, order), jnp.float32), square, pltpu.SemaphoreType.DMA((32,))],
        name="finish",
    )(flags, *arrays)


def sweep(gram):
    row_count = lax.axis_size("row")
    col_count = lax.axis_size("col")
    here_row = lax.axis_index("row")
    here_col = lax.axis_index("col")
    breadth = gram.shape[2]
    mine = gram.astype(jnp.float32).reshape(gram.shape[0] * breadth, breadth)
    first = mine[:breadth]
    odd = here_col % 2 == 1
    pair = here_col // 2
    steps = (col_count // 2).bit_length() - 1
    root = 1

    def send(value, pairs):
        lines = [(a[0] * col_count + a[1], b[0] * col_count + b[1]) for a, b in pairs]
        return lax.ppermute(value, ("row", "col"), lines)

    def swap(value):
        pairs = [((r, c), (r, c ^ 1)) for r in range(row_count) for c in range(col_count)]
        return send(value, pairs)

    def after(value, *others):
        return lax.optimization_barrier((value,) + others)[0]

    def along_row(value, which, *earlier):
        held = value
        for step in range(steps):
            pairs = []
            takes = jnp.zeros((), jnp.bool_)
            for parity in range(2):
                done = list(range(step)) if parity == 0 else list(range(steps - step, steps))
                bit = step if parity == 0 else steps - 1 - step
                targets = []
                for number in range(col_count // 2):
                    if all(number >> b & 1 == 0 for b in range(steps) if b not in done):
                        target = number | 1 << bit
                        targets.append(target)
                        for r in which:
                            pairs.append(((r, 2 * number + parity), (r, 2 * target + parity)))
                for target in targets:
                    takes = takes | (here_col == 2 * target + parity)
            got = send(held, pairs)
            if step == 0 and earlier:
                got = after(got, *earlier)
            held = jnp.where(takes, got, held)
        return held

    def along_column(value, columns, *earlier):
        result = after(value, *earlier) if earlier else value
        for chain in (range(root, 0, -1), range(root, row_count - 1)):
            held = value
            for r in chain:
                upward = chain.step < 0
                target = r - 1 if upward else r + 1
                held = send(held, [((r, c), (target, c)) for c in columns])
                result = jnp.where(here_row == target, held, result)
        return result

    others = range(2, col_count)
    sibling = swap(first)
    across = send(
        jnp.where((here_col == 1) & (here_row == 0), sibling, first),
        [((0, c), (1, c)) for c in range(col_count)] + [((1, c), (0, c)) for c in others],
    )

    at_root = (here_row == root) & (pair == 0)
    flags = jnp.stack([at_root.astype(jnp.int32), odd.astype(jnp.int32)])
    half = breadth // 2
    square = (breadth, breadth)
    lefts, ng, t = pivot_call(
        first_kernel,
        flags,
        mine,
        sibling,
        [mine.shape, square, square],
        [pltpu.VMEM(mine.shape, jnp.float32), pltpu.SemaphoreType.DMA((4,))],
    )
    (s_half,) = pivot_call(second_kernel, flags, t, across, [(half, breadth)])

    lefts = along_row(lefts, range(row_count))
    lefts_sibling = swap(lefts)

    own_row = here_col % row_count
    slot = here_col // row_count
    near = [c for c in others if c % row_count < 2]
    far = [c for c in others if c % row_count >= 2]
    is_far = (own_row >= 2) & (here_col >= 2)
    down_near = jnp.concatenate([across, first], axis=0)
    passed = send(down_near, [((1, c), (2, c)) for c in near])
    pack_flags = jnp.stack(
        [(is_far & (here_row == own_row)).astype(jnp.int32), slot, odd.astype(jnp.int32)]
    )
    packed = pack(pack_flags, lefts, lefts_sibling, passed)
    if row_count == 4:
        pairs = [((2, c), (3, c)) for c in near]
        pairs += [((c % row_count, c), (5 - c % row_count, c)) for c in far]
        later = send(packed, pairs)
    else:
        held = passed
        for r in range(2, row_count - 1):
            passed = send(passed, [((r, c), (r + 1, c)) for c in near])
            held = jnp.where(here_row == r + 1, passed, held)
        passed = held
        later = packed
        for sign in (1, -1):
            moving = packed
            for step in range(row_count - 3):
                pairs = []
                for c in far:
                    source = c % row_count + sign * step
                    if 2 <= source < row_count and 2 <= source + sign < row_count:
                        pairs.append(((source, c), (source + sign, c)))
                moving = send(moving, pairs)
                later = jnp.where(here_row == own_row + sign * (step + 1), moving, later)
    kind = jnp.where(here_row == 2, NEAR, LATER if row_count == 4 else NEAR)
    kind = jnp.where(is_far & (here_row >= 2), jnp.where(here_row == own_row, PACKED, FAR), kind)
    kind = jnp.where(here_row == 0, TOP, jnp.where(here_row == 1, BOTTOM, kind))
    kind = jnp.where(here_col == 0, FIRST, jnp.where(here_col == 1, SECOND, kind))

    ng = along_column(ng, range(2))
    chained = ng
    ng = along_row(ng, [r for r in range(row_count) if r != root], packed)
    ng_sibling = swap(ng)
    pivotal = here_col < 2
    s_root = along_row(s_half, [root])
    s_half = along_column(s_half, range(2), chained)
    s_half = along_row(s_half, [r for r in range(row_count) if r != root])
    s_half = jnp.where(here_row == root, s_root, s_half)
    s_sibling = swap(s_half)
    tests = [kind, odd, here_row == root, pivotal, here_row == 0]
    finish_flags = jnp.stack([test.astype(jnp.int32) for test in tests])
    out = finish(
        finish_flags,
        mine, lefts, lefts_sibling, across, passed, later, packed, ng, ng_sibling,
        s_half, s_sibling,
    )
    return out.reshape(gram.shape)


def solution(mesh):
    placed = (P(None, "row", None, None, "col", None),)
    return jax.shard_map(
        sweep,
        mesh=mesh,
        in_specs=placed,
        out_specs=P(None, "row", None, None, "col", None),
        check_vma=False,
    )
```

profile of v0, /device:TPU:23, one launch (start us, length us, event | category | flops | bytes accessed | tf_op | source)
XLA Modules:
  0.0 132.6 jit_solution(11872786643034855807)
XLA Ops:
  4.4 3.0 %shard_map.17 = (f32[768,384]{1,0:T(8,128)}, f32[384,384]{1,0:T(8,128)}, f32[384,384]{1,0:T(8,128)}) custom-call(s32[2]{0:T(128)} %pad_add_fusion.flags, f32[768,384]{1,0:T(8,128)} %bitcast.14, f32[384,384]{1,0:T(8,128)} %copy-done.7), custom_call_target="tpu_custom_call" | custom-call | tf_op jit(solution)/shard_map/pallas_call | solution.py:177
  8.2 2.5 %broadcast_select_fusion = f32[768,384]{1,0:T(8,128)} fusion(f32[768,384]{1,0:T(8,128)S(1)} %collective-permute-done.1, f32[768,384]{1,0:T(8,128)} %get-tuple-element.10, pred[]{:T(512)S(6)} %or.11), kind=kLoop, calls=%fused_computation.3 | loop fusion | flops 294912 | bytes 3538945 | tf_op jit(solution)/shard_map/jit(_where)/select_n | solution.py:381
  10.7 1.4 %collective-permute-start.2 = (f32[768,384]{1,0:T(8,128)}, f32[768,384]{1,0:T(8,128)}, u32[]{:S(2)}, u32[]{:S(2)}) collective-permute-start(f32[768,384]{1,0:T(8,128)} %broadcast_select_fusion), channel_id=1, source_target_pairs={{0,4},{8,12},{16,20},{24,28},{2,6},{10,14},{18,22},{26,30},{1,3},{... | collective-permute-start | bytes 3538952 | tf_op jit(solution)/shard_map/ppermute | solution.py:352
  13.7 1.5 %collective-permute-start.7 = (f32[384,384]{1,0:T(8,128)S(1)}, f32[384,384]{1,0:T(8,128)}, u32[]{:S(2)}, u32[]{:S(2)}) collective-permute-start(f32[384,384]{1,0:T(8,128)S(1)} %copy-done.12), channel_id=1, source_target_pairs={{8,16},{9,17}} | collective-permute-start | bytes 1769480 | tf_op jit(solution)/shard_map/ppermute | solution.py:352
  15.2 1.5 %collective-permute-start.9 = (f32[384,384]{1,0:T(8,128)S(1)}, f32[384,384]{1,0:T(8,128)}, u32[]{:S(2)}, u32[]{:S(2)}) collective-permute-start(f32[384,384]{1,0:T(8,128)S(1)} %copy-done.12), channel_id=1, source_target_pairs={{8,0},{9,1}} | collective-permute-start | bytes 1769480 | tf_op jit(solution)/shard_map/ppermute | solution.py:352
  16.7 1.2 pad_maximum_fusion
  18.7 1.5 %collective-permute-start.8 = (f32[384,384]{1,0:T(8,128)}, f32[384,384]{1,0:T(8,128)}, u32[]{:S(2)}, u32[]{:S(2)}) collective-permute-start(f32[384,384]{1,0:T(8,128)} %collective-permute-done.7), channel_id=1, source_target_pairs={{16,24},{17,25}} | collective-permute-start | bytes 1769480 | tf_op jit(solution)/shard_map/ppermute | solution.py:352
  20.1 21.4 %collective-permute-done.2 = f32[768,384]{1,0:T(8,128)} collective-permute-done((f32[768,384]{1,0:T(8,128)}, f32[768,384]{1,0:T(8,128)}, u32[]{:S(2)}, u32[]{:S(2)}) %collective-permute-start.2) | collective-permute-done | bytes 1179680 | tf_op jit(solution)/shard_map/ppermute | solution.py:352
  41.5 1.4 %broadcast_select_fusion.1.lefts = f32[768,384]{1,0:T(8,128)S(1)} fusion(f32[768,384]{1,0:T(8,128)} %collective-permute-done.2, f32[768,384]{1,0:T(8,128)} %broadcast_select_fusion, pred[]{:T(512)S(6)} %or.10), kind=kLoop, calls=%fused_computation.4 | loop fusion | flops 294912 | bytes 3538945 | tf_op jit(solution)/shard_map/jit(_where)/select_n | solution.py:381
  43.0 2.1 %collective-permute-start.3 = (f32[768,384]{1,0:T(8,128)S(1)}, f32[768,384]{1,0:T(8,128)}, u32[]{:S(2)}, u32[]{:S(2)}) collective-permute-start(f32[768,384]{1,0:T(8,128)S(1)} %broadcast_select_fusion.1.lefts), channel_id=1, source_target_pairs={{0,1},{1,0},{2,3},{3,2},{4,5},{5,4},{6,7},{7,6},{8,9},{9,8},{10,11... | collective-permute-start | bytes 3538952 | tf_op jit(solution)/shard_map/ppermute | solution.py:352
  45.1 1.2 select_select_fusion
  47.7 1.4 %collective-permute-start.15 = (f32[192,384]{1,0:T(8,128)}, f32[192,384]{1,0:T(8,128)}, u32[]{:S(2)}, u32[]{:S(2)}) collective-permute-start(f32[192,384]{1,0:T(8,128)} %shard_map.18), channel_id=1, source_target_pairs={{8,16},{9,17}} | collective-permute-start | bytes 884744 | tf_op jit(solution)/shard_map/ppermute | solution.py:352
  49.1 1.4 %collective-permute-start.17 = (f32[192,384]{1,0:T(8,128)}, f32[192,384]{1,0:T(8,128)}, u32[]{:S(2)}, u32[]{:S(2)}) collective-permute-start(f32[192,384]{1,0:T(8,128)} %shard_map.18), channel_id=1, source_target_pairs={{8,0},{9,1}} | collective-permute-start | bytes 884744 | tf_op jit(solution)/shard_map/ppermute | solution.py:352
  50.5 1.4 %collective-permute-start.16 = (f32[192,384]{1,0:T(8,128)}, f32[192,384]{1,0:T(8,128)}, u32[]{:S(2)}, u32[]{:S(2)}) collective-permute-start(f32[192,384]{1,0:T(8,128)} %collective-permute-done.15), channel_id=1, source_target_pairs={{16,24},{17,25}} | collective-permute-start | bytes 884744 | tf_op jit(solution)/shard_map/ppermute | solution.py:352
  52.4 1.4 %collective-permute-start.13 = (f32[192,384]{1,0:T(8,128)}, f32[192,384]{1,0:T(8,128)}, u32[]{:S(2)}, u32[]{:S(2)}) collective-permute-start(f32[192,384]{1,0:T(8,128)} %shard_map.18), channel_id=1, source_target_pairs={{8,10},{9,13}} | collective-permute-start | bytes 884744 | tf_op jit(solution)/shard_map/ppermute | solution.py:352
  53.8 3.0 %pack.1.packed = f32[768,384]{1,0:T(8,128)} custom-call(s32[3]{0:T(128)} %pad_add_fusion.1.flags, f32[768,384]{1,0:T(8,128)} %copy-done.2, f32[768,384]{1,0:T(8,128)} %collective-permute-done.3.sibling, f32[768,384]{1,0:T(8,128)} %copy-done.4), custom_call_target="tpu_custom_call" | custom-call | tf_op jit(solution)/shard_map/pack/pallas_call | solution.py:227
  56.9 1.4 %collective-permute-start.11 = (f32[384,384]{1,0:T(8,128)S(1)}, f32[384,384]{1,0:T(8,128)S(1)}, u32[]{:S(2)}, u32[]{:S(2)}) collective-permute-start(f32[384,384]{1,0:T(8,128)S(1)} %broadcast_select_fusion.2), channel_id=1, source_target_pairs={{0,4},{16,20},{24,28},{2,6},{18,22},{26,30},{1,3},{17,19},{25,27},... | collective-permute-start | bytes 1769480 | tf_op jit(solution)/shard_map/ppermute | solution.py:352
  60.3 1.3 collective-permute-start.6
  62.4 1.3 collective-permute-start.19
  63.7 28.4 %collective-permute-done.11 = f32[384,384]{1,0:T(8,128)S(1)} collective-permute-done((f32[384,384]{1,0:T(8,128)S(1)}, f32[384,384]{1,0:T(8,128)S(1)}, u32[]{:S(2)}, u32[]{:S(2)}) %collective-permute-start.11) | collective-permute-done | bytes 589856 | tf_op jit(solution)/shard_map/ppermute | solution.py:352
  92.2 3.7 %collective-permute-start.12 = (f32[384,384]{1,0:T(8,128)S(1)}, f32[384,384]{1,0:T(8,128)}, u32[]{:S(2)}, u32[]{:S(2)}) collective-permute-start(f32[384,384]{1,0:T(8,128)S(1)} %broadcast_select_fusion.3.ng), channel_id=1, source_target_pairs={{0,1},{1,0},{2,3},{3,2},{4,5},{5,4},{6,7},{7,6},{8,9},{9,8},{10,11... | collective-permute-start | bytes 1769480 | tf_op jit(solution)/shard_map/ppermute | solution.py:352
  95.8 22.5 %collective-permute-done.19 = f32[192,384]{1,0:T(8,128)S(1)} collective-permute-done((f32[192,384]{1,0:T(8,128)S(1)}, f32[192,384]{1,0:T(8,128)S(1)}, u32[]{:S(2)}, u32[]{:S(2)}) %collective-permute-start.19) | collective-permute-done | bytes 294944 | tf_op jit(solution)/shard_map/ppermute | solution.py:352
  118.3 1.8 %collective-permute-start.20 = (f32[192,384]{1,0:T(8,128)S(1)}, f32[192,384]{1,0:T(8,128)S(1)}, u32[]{:S(2)}, u32[]{:S(2)}) collective-permute-start(f32[192,384]{1,0:T(8,128)S(1)} %select_select_fusion.1.s_mine), channel_id=1, source_target_pairs={{0,1},{1,0},{2,3},{3,2},{4,5},{5,4},{6,7},{7,6},{8,9},{9,8},{10,11... | collective-permute-start | bytes 884744 | tf_op jit(solution)/shard_map/ppermute | solution.py:352
  123.1 9.4 %finish.1 = f32[2304,128]{1,0:T(8,128)} custom-call(s32[5]{0:T(128)} %stack.62.flags, f32[768,384]{1,0:T(8,128)} %bitcast.15, f32[768,384]{1,0:T(8,128)} %copy-done.2, f32[768,384]{1,0:T(8,128)} %collective-permute-done.3.sibling, f32[384,384]{1,0:T(8,128)} %copy-done.3, f32[768,384]{1,0:T(8,128)} %copy-done.4, f32[768,384]{1,0:T(8,128)} %copy-done.11, ...), custom_call_target="tpu_custom_call" | custom-call | tf_op jit(solution)/shard_map/finish/pallas_call | solution.py:326
  (66 shorter events, 15.2 us)
Async XLA Ops:
  1.2 2.4 %collective-permute-start = (f32[384,384]{1,0:T(8,128)S(1)}, f32[384,384]{1,0:T(8,128)S(1)}, u32[]{:S(2)}, u32[]{:S(2)}) collective-permute-start(f32[384,384]{1,0:T(8,128)S(1)} %slice_bitcast_fusion), channel_id=1, source_target_pairs={{0,1},{1,0},{2,3},{3,2},{4,5},{5,4},{6,7},{7,6},{8,9},{9,8},{10,11... | collective-permute-start | bytes 1769480 | tf_op jit(solution)/shard_map/ppermute | solution.py:352
  7.4 0.8 collective-permute-start.1
  8.1 4.0 %copy-start.1 = (f32[2,1,384,1,1,384]{5,2,4,3,1,0:T(8,128)S(1)}, f32[2,1,384,1,1,384]{5,2,4,3,1,0:T(8,128)}, u32[]{:S(2)}) copy-start(f32[2,1,384,1,1,384]{5,2,4,3,1,0:T(8,128)} %copy-done) | copy-start | bytes 3538948
  10.7 30.8 %collective-permute-start.2 = (f32[768,384]{1,0:T(8,128)}, f32[768,384]{1,0:T(8,128)}, u32[]{:S(2)}, u32[]{:S(2)}) collective-permute-start(f32[768,384]{1,0:T(8,128)} %broadcast_select_fusion), channel_id=1, source_target_pairs={{0,4},{8,12},{16,20},{24,28},{2,6},{10,14},{18,22},{26,30},{1,3},{... | collective-permute-start | bytes 3538952 | tf_op jit(solution)/shard_map/ppermute | solution.py:352
  13.0 3.7 %collective-permute-start.4 = (f32[384,384]{1,0:T(8,128)}, f32[384,384]{1,0:T(8,128)S(1)}, u32[]{:S(2)}, u32[]{:S(2)}) collective-permute-start(f32[384,384]{1,0:T(8,128)} %broadcast_select_fusion.4), channel_id=1, source_target_pairs={{0,8},{1,9},{2,10},{3,11},{4,12},{5,13},{6,14},{7,15},{10,2},{11,3... | collective-permute-start | bytes 1769480 | tf_op jit(solution)/shard_map/ppermute | solution.py:352
  13.7 4.9 %collective-permute-start.7 = (f32[384,384]{1,0:T(8,128)S(1)}, f32[384,384]{1,0:T(8,128)}, u32[]{:S(2)}, u32[]{:S(2)}) collective-permute-start(f32[384,384]{1,0:T(8,128)S(1)} %copy-done.12), channel_id=1, source_target_pairs={{8,16},{9,17}} | collective-permute-start | bytes 1769480 | tf_op jit(solution)/shard_map/ppermute | solution.py:352
  15.2 29.9 %collective-permute-start.9 = (f32[384,384]{1,0:T(8,128)S(1)}, f32[384,384]{1,0:T(8,128)}, u32[]{:S(2)}, u32[]{:S(2)}) collective-permute-start(f32[384,384]{1,0:T(8,128)S(1)} %copy-done.12), channel_id=1, source_target_pairs={{8,0},{9,1}} | collective-permute-start | bytes 1769480 | tf_op jit(solution)/shard_map/ppermute | solution.py:352
  16.7 26.2 %copy-start.3 = (f32[384,384]{1,0:T(8,128)}, f32[384,384]{1,0:T(8,128)S(1)}, u32[]{:S(2)}) copy-start(f32[384,384]{1,0:T(8,128)S(1)} %collective-permute-done.4.a00.across) | copy-start | bytes 1769476
  17.9 34.5 %collective-permute-start.5 = (f32[768,384]{1,0:T(8,128)}, f32[768,384]{1,0:T(8,128)S(1)}, u32[]{:S(2)}, u32[]{:S(2)}) collective-permute-start(f32[768,384]{1,0:T(8,128)} %pad_maximum_fusion), channel_id=1, source_target_pairs={{12,20},{13,21}} | collective-permute-start | bytes 3538952 | tf_op jit(solution)/shard_map/ppermute | solution.py:352
  18.7 26.4 %collective-permute-start.8 = (f32[384,384]{1,0:T(8,128)}, f32[384,384]{1,0:T(8,128)}, u32[]{:S(2)}, u32[]{:S(2)}) collective-permute-start(f32[384,384]{1,0:T(8,128)} %collective-permute-done.7), channel_id=1, source_target_pairs={{16,24},{17,25}} | collective-permute-start | bytes 1769480 | tf_op jit(solution)/shard_map/ppermute | solution.py:352
  43.0 10.8 %collective-permute-start.3 = (f32[768,384]{1,0:T(8,128)S(1)}, f32[768,384]{1,0:T(8,128)}, u32[]{:S(2)}, u32[]{:S(2)}) collective-permute-start(f32[768,384]{1,0:T(8,128)S(1)} %broadcast_select_fusion.1.lefts), channel_id=1, source_target_pairs={{0,1},{1,0},{2,3},{3,2},{4,5},{5,4},{6,7},{7,6},{8,9},{9,8},{10,11... | collective-permute-start | bytes 3538952 | tf_op jit(solution)/shard_map/ppermute | solution.py:352
  46.3 10.5 %collective-permute-start.10 = (f32[384,384]{1,0:T(8,128)S(1)}, f32[384,384]{1,0:T(8,128)S(1)}, u32[]{:S(2)}, u32[]{:S(2)}) collective-permute-start(f32[384,384]{1,0:T(8,128)S(1)} %select_select_fusion), channel_id=1, source_target_pairs={{0,2},{16,18},{24,26},{1,5},{17,21},{25,29}} | collective-permute-start | bytes 1769480 | tf_op jit(solution)/shard_map/ppermute | solution.py:352
  47.7 2.8 %collective-permute-start.15 = (f32[192,384]{1,0:T(8,128)}, f32[192,384]{1,0:T(8,128)}, u32[]{:S(2)}, u32[]{:S(2)}) collective-permute-start(f32[192,384]{1,0:T(8,128)} %shard_map.18), channel_id=1, source_target_pairs={{8,16},{9,17}} | collective-permute-start | bytes 884744 | tf_op jit(solution)/shard_map/ppermute | solution.py:352
  49.1 9.3 %collective-permute-start.17 = (f32[192,384]{1,0:T(8,128)}, f32[192,384]{1,0:T(8,128)}, u32[]{:S(2)}, u32[]{:S(2)}) collective-permute-start(f32[192,384]{1,0:T(8,128)} %shard_map.18), channel_id=1, source_target_pairs={{8,0},{9,1}} | collective-permute-start | bytes 884744 | tf_op jit(solution)/shard_map/ppermute | solution.py:352
  50.5 7.9 %collective-permute-start.16 = (f32[192,384]{1,0:T(8,128)}, f32[192,384]{1,0:T(8,128)}, u32[]{:S(2)}, u32[]{:S(2)}) collective-permute-start(f32[192,384]{1,0:T(8,128)} %collective-permute-done.15), channel_id=1, source_target_pairs={{16,24},{17,25}} | collective-permute-start | bytes 884744 | tf_op jit(solution)/shard_map/ppermute | solution.py:352
  52.4 9.2 %collective-permute-start.13 = (f32[192,384]{1,0:T(8,128)}, f32[192,384]{1,0:T(8,128)}, u32[]{:S(2)}, u32[]{:S(2)}) collective-permute-start(f32[192,384]{1,0:T(8,128)} %shard_map.18), channel_id=1, source_target_pairs={{8,10},{9,13}} | collective-permute-start | bytes 884744 | tf_op jit(solution)/shard_map/ppermute | solution.py:352
  56.9 35.2 %collective-permute-start.11 = (f32[384,384]{1,0:T(8,128)S(1)}, f32[384,384]{1,0:T(8,128)S(1)}, u32[]{:S(2)}, u32[]{:S(2)}) collective-permute-start(f32[384,384]{1,0:T(8,128)S(1)} %broadcast_select_fusion.2), channel_id=1, source_target_pairs={{0,4},{16,20},{24,28},{2,6},{18,22},{26,30},{1,3},{17,19},{25,27},... | collective-permute-start | bytes 1769480 | tf_op jit(solution)/shard_map/ppermute | solution.py:352
  59.4 2.9 %collective-permute-start.18 = (f32[192,384]{1,0:T(8,128)S(1)}, f32[192,384]{1,0:T(8,128)S(1)}, u32[]{:S(2)}, u32[]{:S(2)}) collective-permute-start(f32[192,384]{1,0:T(8,128)S(1)} %select_select_fusion.2), channel_id=1, source_target_pairs={{0,2},{16,18},{24,26},{1,5},{17,21},{25,29}} | collective-permute-start | bytes 884744 | tf_op jit(solution)/shard_map/ppermute | solution.py:352
  60.3 61.1 %collective-permute-start.6 = (f32[768,384]{1,0:T(8,128)S(1)}, f32[768,384]{1,0:T(8,128)S(1)}, u32[]{:S(2)}, u32[]{:S(2)}) collective-permute-start(f32[768,384]{1,0:T(8,128)S(1)} %copy-done.5), channel_id=1, source_target_pairs={{20,28},{21,29},{18,26},{27,19},{22,30},{31,23}} | collective-permute-start | bytes 3538952 | tf_op jit(solution)/shard_map/ppermute | solution.py:352
  61.7 34.2 %collective-permute-start.14 = (f32[192,384]{1,0:T(8,128)S(1)}, f32[192,384]{1,0:T(8,128)S(1)}, u32[]{:S(2)}, u32[]{:S(2)}) collective-permute-start(f32[192,384]{1,0:T(8,128)S(1)} %broadcast_select_fusion.6), channel_id=1, source_target_pairs={{8,12},{10,14},{9,11},{13,15}} | collective-permute-start | bytes 884744 | tf_op jit(solution)/shard_map/ppermute | solution.py:352
  62.4 55.9 %collective-permute-start.19 = (f32[192,384]{1,0:T(8,128)S(1)}, f32[192,384]{1,0:T(8,128)S(1)}, u32[]{:S(2)}, u32[]{:S(2)}) collective-permute-start(f32[192,384]{1,0:T(8,128)S(1)} %broadcast_select_fusion.5), channel_id=1, source_target_pairs={{0,4},{16,20},{24,28},{2,6},{18,22},{26,30},{1,3},{17,19},{25,27},... | collective-permute-start | bytes 884744 | tf_op jit(solution)/shard_map/ppermute | solution.py:352
  92.1 29.2 %copy-start.9 = (f32[384,384]{1,0:T(8,128)}, f32[384,384]{1,0:T(8,128)S(1)}, u32[]{:S(2)}) copy-start(f32[384,384]{1,0:T(8,128)S(1)} %broadcast_select_fusion.3.ng) | copy-start | bytes 1769476
  92.2 29.2 %collective-permute-start.12 = (f32[384,384]{1,0:T(8,128)S(1)}, f32[384,384]{1,0:T(8,128)}, u32[]{:S(2)}, u32[]{:S(2)}) collective-permute-start(f32[384,384]{1,0:T(8,128)S(1)} %broadcast_select_fusion.3.ng), channel_id=1, source_target_pairs={{0,1},{1,0},{2,3},{3,2},{4,5},{5,4},{6,7},{7,6},{8,9},{9,8},{10,11... | collective-permute-start | bytes 1769480 | tf_op jit(solution)/shard_map/ppermute | solution.py:352
  118.3 3.0 %collective-permute-start.20 = (f32[192,384]{1,0:T(8,128)S(1)}, f32[192,384]{1,0:T(8,128)S(1)}, u32[]{:S(2)}, u32[]{:S(2)}) collective-permute-start(f32[192,384]{1,0:T(8,128)S(1)} %select_select_fusion.1.s_mine), channel_id=1, source_target_pairs={{0,1},{1,0},{2,3},{3,2},{4,5},{5,4},{6,7},{7,6},{8,9},{9,8},{10,11... | collective-permute-start | bytes 884744 | tf_op jit(solution)/shard_map/ppermute | solution.py:352
  (11 other events, 24.7 us)
where the time goes:
time: 133 us
  waiting for transfers between devices  73.9 us (56%)
  starting transfers between devices  28.1 us (21%)
  Pallas kernels  16.1 us (12%)
  other arithmetic  10.8 us (8%)
  local copies, waits for them, and re-layouts  3.28 us (2%)
    ppermute x21, waiting for transfers between devices, send(): return lax.ppermute(value, ('row', 'col'), lines)  73.9 us
    ppermute x21, starting transfers between devices, send(): return lax.ppermute(value, ('row', 'col'), lines)  28.1 us
    pallas_call x1, Pallas kernels, finish(): pl.pallas_call(finish_kernel, out_shape=jax.ShapeDtypeStruct(linear, jnp....  9.37 us
    select_n x6, other arithmetic, along_row(): held = jnp.where(takes, got, held)  4.14 us
    pallas_call x2, Pallas kernels, pivot_call(): pl.pallas_call(kernel, out_shape=[jax.ShapeDtypeStruct(shape, jnp.float32...  3.67 us
    pallas_call x1, Pallas kernels, pack(): pl.pallas_call(pack_kernel, out_shape=jax.ShapeDtypeStruct(near.shape, jn...  3.02 us
  transfers between devices with their start and end apart: 21, of which 5 were waited for; matrix products, arithmetic and copies ran while one was open for 6% of the time, Pallas kernels for 3%

commit v1 on v0

--- a/solution.py
+++ b/solution.py
@@ -38,9 +38,9 @@
             left = ref[:, lanes]
             inside = (lanes_left >= lower) & (lanes_left < lower + LEAF)
             high, middle, low = split(jnp.where(inside, left, 0.0))
-            twice = high + pltpu.roll(middle, LEAF, 1)
-            packed = twice + pltpu.roll(twice, 2 * LEAF, 1)
-            packed = packed + pltpu.roll(high, 4 * LEAF, 1) + pltpu.roll(low, 5 * LEAF, 1)
+            packed = high + pltpu.roll(middle, LEAF, 1)
+            packed = packed + (pltpu.roll(high, 2 * LEAF, 1) + pltpu.roll(middle, 3 * LEAF, 1))
+            packed = packed + (pltpu.roll(high, 4 * LEAF, 1) + pltpu.roll(low, 5 * LEAF, 1))
             left_ref[...] = packed.astype(jnp.bfloat16)
             ref[:, lanes] = jnp.where(inside, 0.0, left)
             columns = [
@@ -95,6 +95,11 @@
     return raw_dot(left, right, contract)
 
 
+def pieces(value):
+    high = value.astype(jnp.bfloat16)
+    return high, (value - high.astype(jnp.float32)).astype(jnp.bfloat16)
+
+
 def halves(value):
     return [part.astype(jnp.bfloat16) for part in split(value)]
 
@@ -152,13 +157,23 @@
             copy.wait()
 
 
-def second_kernel(flags, t, a00, s_out, s_ref, a_ref, left_ref, semaphore):
+def second_kernel(
+    flags, t, across, first, s_out, near_out, s_ref, a_ref, left_ref, semaphore
+):
+    order = a_ref.shape[0]
     half = s_out.shape[0]
 
+    @pl.when(flags[2] != 0)
+    def _():
+        fetch(across, s_ref, semaphore)
+        fetch(first, a_ref, semaphore)
+        fetch(s_ref, near_out.at[pl.ds(0, order)], semaphore)
+        fetch(a_ref, near_out.at[pl.ds(order, order)], semaphore)
+
     @pl.when(flags[0] != 0)
     def _():
         fetch(t, a_ref, semaphore)
-        fetch(a00, s_ref, semaphore)
+        fetch(across, s_ref, semaphore)
         s_ref[...] = s_ref[...] - a_ref[...]
         invert(s_ref, left_ref)
 
@@ -171,13 +186,13 @@
             fetch(s_ref.at[pl.ds(0, half)], s_out, semaphore)
 
 
-def pivot_call(kernel, flags, left, right, outs, more=()):
-    order = right.shape[0]
+def pivot_call(kernel, flags, arrays, outs, more=()):
+    order = arrays[1].shape[0]
     anywhere = pl.BlockSpec(memory_space=pl.ANY)
     return pl.pallas_call(
         kernel,
         out_shape=[jax.ShapeDtypeStruct(shape, jnp.float32) for shape in outs],
-        in_specs=[pl.BlockSpec(memory_space=pltpu.SMEM), anywhere, anywhere],
+        in_specs=[pl.BlockSpec(memory_space=pltpu.SMEM)] + [anywhere] * len(arrays),
         out_specs=[anywhere] * len(outs),
         scratch_shapes=[
             pltpu.VMEM((order, order), jnp.float32),
@@ -186,7 +201,7 @@
             pltpu.SemaphoreType.DMA,
             *more,
         ],
-    )(flags, left, right)
+    )(flags, *arrays)
 
 
 def transfer(cases, semaphores, begin, place=0):
@@ -208,9 +223,9 @@
     order = out.shape[0] // 2
     at = pl.ds(pl.multiple_of(flags[1] * order, order), order)
     head, tail = pl.ds(0, order), pl.ds(order, order)
-    far, odd = flags[0] != 0, flags[2] != 0
+    far, odd, close = flags[0] != 0, flags[2] != 0, flags[3] != 0
     cases = [
-        (jnp.logical_not(far), [(near, held)]),
+        (close, [(near, held)]),
         (far & odd, [(sibling.at[at], held.at[head]), (lefts.at[at], held.at[tail])]),
         (
             far & jnp.logical_not(odd),
@@ -219,7 +234,10 @@
     ]
     transfer(cases, semaphores, True)
     transfer(cases, semaphores, False)
-    fetch(held, out, semaphores.at[0])
+
+    @pl.when(far | close)
+    def _():
+        fetch(held, out, semaphores.at[0])
 
 
 def pack(flags, lefts, sibling, near):
@@ -237,7 +255,7 @@
 FIRST, SECOND, TOP, BOTTOM, NEAR, FAR, PACKED, LATER = range(8)
 
 
-PRODUCTS = ((0, 2), (2, 0), (1, 1), (0, 1), (1, 0), (0, 0))
+PRODUCTS = ((0, 1), (1, 0), (0, 0))
 
 
 def finish_kernel(
@@ -288,19 +306,19 @@
         r_ref[tail, :] = jnp.where(kind == FIRST, 0.0, unit)
 
     r1 = r_ref[tail, :].astype(jnp.bfloat16)
-    g = halves(g_ref[...])
-    n = halves(n_ref[...])
-    s = halves(s_ref[...])
-    y = halves(r_ref[head, :] - joined([(part, r1) for part in reversed(g)], (0, 0)))
+    g, n, s = [pieces(ref[...]) for ref in (g_ref, n_ref, s_ref)]
+    y = pieces(r_ref[head, :] - joined([(part, r1) for part in reversed(g)], (0, 0)))
     w0 = joined([(s[i], y[j]) for i, j in PRODUCTS])
-    w = halves(w0)
+    w = pieces(w0)
     w1 = joined([(part, r1) for part in reversed(n)])
     w1 = w1 - joined([(g[i], w[j]) for i, j in PRODUCTS])
-    v = halves(w1)
+    v = pieces(w1)
     transfer(second, semaphores, False, place)
     left0 = left0_ref[...].astype(jnp.bfloat16)
     left1 = left1_ref[...].astype(jnp.bfloat16)
-    change = joined([(left0, w[i]) for i in (2, 1, 0)] + [(left1, v[i]) for i in (2, 1, 0)])
+    sides = [jnp.concatenate(parts, axis=1) for parts in (w, v)]
+    both = joined([(left0, sides[0]), (left1, sides[1])])
+    change = both[:, order:] + both[:, :order]
     mine_ref[...] = jnp.where(pivotal, 0.0, mine_ref[...]) - change
 
     @pl.when(in_top)
@@ -400,18 +418,20 @@
     )
 
     at_root = (here_row == root) & (pair == 0)
-    flags = jnp.stack([at_root.astype(jnp.int32), odd.astype(jnp.int32)])
+    to_near = (here_row == 1) & (here_col >= 2) & (here_col % row_count < 2)
+    flags = jnp.stack([test.astype(jnp.int32) for test in (at_root, odd, to_near)])
     half = breadth // 2
     square = (breadth, breadth)
     lefts, ng, t = pivot_call(
         first_kernel,
         flags,
-        mine,
-        sibling,
+        [mine, sibling],
         [mine.shape, square, square],
         [pltpu.VMEM(mine.shape, jnp.float32), pltpu.SemaphoreType.DMA((4,))],
     )
-    (s_half,) = pivot_call(second_kernel, flags, t, across, [(half, breadth)])
+    s_half, down_near = pivot_call(
+        second_kernel, flags, [t, across, first], [(half, breadth), mine.shape]
+    )
 
     lefts = along_row(lefts, range(row_count))
     lefts_sibling = swap(lefts)
@@ -421,11 +441,10 @@
     near = [c for c in others if c % row_count < 2]
     far = [c for c in others if c % row_count >= 2]
     is_far = (own_row >= 2) & (here_col >= 2)
-    down_near = jnp.concatenate([across, first], axis=0)
     passed = send(down_near, [((1, c), (2, c)) for c in near])
-    pack_flags = jnp.stack(
-        [(is_far & (here_row == own_row)).astype(jnp.int32), slot, odd.astype(jnp.int32)]
-    )
+    is_close = (here_row == 2) & (own_row < 2) & (here_col >= 2)
+    tests = [is_far & (here_row == own_row), slot, odd, is_close]
+    pack_flags = jnp.stack([test.astype(jnp.int32) for test in tests])
     packed = pack(pack_flags, lefts, lefts_sibling, passed)
     if row_count == 4:
         pairs = [((2, c), (3, c)) for c in near]

time: 133 us -> 131 us (0.985)
  Pallas kernels: 16.1 us -> 11.7 us
  waiting for transfers between devices: 73.9 us -> 71 us
  local copies, waits for them, and re-layouts: 3.28 us -> 5.09 us
  starting transfers between devices: 28.1 us -> 29.7 us
    ppermute x21, waiting for transfers between devices: 73.9 us -> 71 us  [send(): return lax.ppermute(value, ('row', 'col'), lines)]
    pallas_call x1, Pallas kernels: 3.02 us -> 0.72 us  [pack(): pl.pallas_call(pack_kernel, out_shape=jax.ShapeDtypeStruct(near.shape, jn...]
    pallas_call x1, Pallas kernels: 9.37 us -> 7.33 us  [finish(): pl.pallas_call(finish_kernel, out_shape=jax.ShapeDtypeStruct(linear, jnp....]
    unnamed x28, local copies, waits for them, and re-layouts: 2.58 us -> 4.38 us
    ppermute x21, starting transfers between devices: 28.1 us -> 29.7 us  [send(): return lax.ppermute(value, ('row', 'col'), lines)]
  transfers between devices with their start and end apart: 21 -> 21, of which waited for: 5 -> 5; matrix products, arithmetic and copies ran while one was open for 6% -> 8% of each run, Pallas kernels for 3% -> 1%
where the time goes in v1:
time: 131 us; the launch traced here: 130 us
  waiting for transfers between devices  71 us (54%)
  starting transfers between devices  29.7 us (23%)
  other arithmetic  11.9 us (9%)
  Pallas kernels  11.7 us (9%)
  local copies, waits for them, and re-layouts  5.09 us (4%)
    ppermute x21, waiting for transfers between devices, send(): return lax.ppermute(value, ('row', 'col'), lines)  71 us
    ppermute x21, starting transfers between devices, send(): return lax.ppermute(value, ('row', 'col'), lines)  29.7 us
    pallas_call x1, Pallas kernels, finish(): pl.pallas_call(finish_kernel, out_shape=jax.ShapeDtypeStruct(linear, jnp....  7.33 us
    select_n x6, other arithmetic, along_row(): held = jnp.where(takes, got, held)  5.17 us
    unnamed x28, local copies, waits for them, and re-layouts  4.38 us
    pallas_call x2, Pallas kernels, pivot_call(): pl.pallas_call(kernel, out_shape=[jax.ShapeDtypeStruct(shape, jnp.float32...  3.68 us
    select_n x2, other arithmetic, along_column(): result = jnp.where(here_row == target, held, result)  3.31 us
  transfers between devices with their start and end apart: 21, of which 5 were waited for; matrix products, arithmetic and copies ran while one was open for 8% of the time, Pallas kernels for 1%

profile of v1, /device:TPU:23, one launch (start us, length us, event | category | flops | bytes accessed | tf_op | source)
XLA Modules:
  0.0 129.9 jit_solution(11214301355132199877)
XLA Ops:
  4.4 3.0 %shard_map.17 = (f32[768,384]{1,0:T(8,128)}, f32[384,384]{1,0:T(8,128)}, f32[384,384]{1,0:T(8,128)}) custom-call(s32[3]{0:T(128)} %pad_add_fusion.flags, f32[768,384]{1,0:T(8,128)} %bitcast.16, f32[384,384]{1,0:T(8,128)} %copy-done.7), custom_call_target="tpu_custom_call" | custom-call | tf_op jit(solution)/shard_map/pallas_call | solution.py:192
  7.4 1.7 %collective-permute-start.1 = (f32[768,384]{1,0:T(8,128)}, f32[768,384]{1,0:T(8,128)}, u32[]{:S(2)}, u32[]{:S(2)}) collective-permute-start(f32[768,384]{1,0:T(8,128)} %get-tuple-element.12), channel_id=1, source_target_pairs={{0,2},{8,10},{16,18},{24,26},{1,5},{9,13},{17,21},{25,29}} | collective-permute-start | bytes 3538952 | tf_op jit(solution)/shard_map/ppermute | solution.py:370
  9.1 1.5 %broadcast_select_fusion = f32[768,384]{1,0:T(8,128)S(1)} fusion(f32[768,384]{1,0:T(8,128)} %collective-permute-done.1, f32[768,384]{1,0:T(8,128)} %get-tuple-element.12, pred[]{:T(512)S(6)} %or.11), kind=kLoop, calls=%fused_computation.2 | loop fusion | flops 294912 | bytes 3538945 | tf_op jit(solution)/shard_map/jit(_where)/select_n | solution.py:399
  10.6 1.3 collective-permute-start.2
  13.5 1.5 %collective-permute-start.7 = (f32[384,384]{1,0:T(8,128)}, f32[384,384]{1,0:T(8,128)}, u32[]{:S(2)}, u32[]{:S(2)}) collective-permute-start(f32[384,384]{1,0:T(8,128)} %get-tuple-element.15), channel_id=1, source_target_pairs={{8,16},{9,17}} | collective-permute-start | bytes 1769480 | tf_op jit(solution)/shard_map/ppermute | solution.py:370
  15.0 1.5 %collective-permute-start.9 = (f32[384,384]{1,0:T(8,128)}, f32[384,384]{1,0:T(8,128)}, u32[]{:S(2)}, u32[]{:S(2)}) collective-permute-start(f32[384,384]{1,0:T(8,128)} %get-tuple-element.15), channel_id=1, source_target_pairs={{8,0},{9,1}} | collective-permute-start | bytes 1769480 | tf_op jit(solution)/shard_map/ppermute | solution.py:370
  18.8 1.5 %collective-permute-start.8 = (f32[384,384]{1,0:T(8,128)}, f32[384,384]{1,0:T(8,128)}, u32[]{:S(2)}, u32[]{:S(2)}) collective-permute-start(f32[384,384]{1,0:T(8,128)} %collective-permute-done.7), channel_id=1, source_target_pairs={{16,24},{17,25}} | collective-permute-start | bytes 1769480 | tf_op jit(solution)/shard_map/ppermute | solution.py:370
  20.3 21.3 %collective-permute-done.2 = f32[768,384]{1,0:T(8,128)} collective-permute-done((f32[768,384]{1,0:T(8,128)S(1)}, f32[768,384]{1,0:T(8,128)}, u32[]{:S(2)}, u32[]{:S(2)}) %collective-permute-start.2) | collective-permute-done | bytes 1179680 | tf_op jit(solution)/shard_map/ppermute | solution.py:370
  41.6 1.4 %broadcast_select_fusion.1.lefts = f32[768,384]{1,0:T(8,128)S(1)} fusion(f32[768,384]{1,0:T(8,128)} %collective-permute-done.2, f32[768,384]{1,0:T(8,128)S(1)} %broadcast_select_fusion, pred[]{:T(512)S(6)} %or.10), kind=kLoop, calls=%fused_computation.3 | loop fusion | flops 294912 | bytes 3538945 | tf_op jit(solution)/shard_map/jit(_where)/select_n | solution.py:399
  43.0 2.1 %collective-permute-start.3 = (f32[768,384]{1,0:T(8,128)S(1)}, f32[768,384]{1,0:T(8,128)S(1)}, u32[]{:S(2)}, u32[]{:S(2)}) collective-permute-start(f32[768,384]{1,0:T(8,128)S(1)} %broadcast_select_fusion.1.lefts), channel_id=1, source_target_pairs={{0,1},{1,0},{2,3},{3,2},{4,5},{5,4},{6,7},{7,6},{8,9},{9,8},{10,11... | collective-permute-start | bytes 3538952 | tf_op jit(solution)/shard_map/ppermute | solution.py:370
  45.1 2.2 %select_select_fusion = f32[384,384]{1,0:T(8,128)} fusion(f32[384,384]{1,0:T(8,128)} %collective-permute-done.8, f32[384,384]{1,0:T(8,128)} %collective-permute-done.7, f32[384,384]{1,0:T(8,128)} %collective-permute-done.9, f32[384,384]{1,0:T(8,128)} %get-tuple-element.15, pred[]{:T(512)S(6)} %eq.36, pred[]{:T(512)S(6)} %eq.39, pred[]{:T(512)S(6)} %eq.48), kind=kLoop, calls=%fused_computation.1 | loop fusion | flops 442368 | bytes 2949123 | tf_op jit(solution)/shard_map/jit(_where)/select_n | solution.py:410
  47.3 1.5 %collective-permute-start.10 = (f32[384,384]{1,0:T(8,128)}, f32[384,384]{1,0:T(8,128)}, u32[]{:S(2)}, u32[]{:S(2)}) collective-permute-start(f32[384,384]{1,0:T(8,128)} %select_select_fusion), channel_id=1, source_target_pairs={{0,2},{16,18},{24,26},{1,5},{17,21},{25,29}} | collective-permute-start | bytes 1769480 | tf_op jit(solution)/shard_map/ppermute | solution.py:370
  48.8 1.4 %collective-permute-start.15 = (f32[192,384]{1,0:T(8,128)}, f32[192,384]{1,0:T(8,128)}, u32[]{:S(2)}, u32[]{:S(2)}) collective-permute-start(f32[192,384]{1,0:T(8,128)} %get-tuple-element.18), channel_id=1, source_target_pairs={{8,16},{9,17}} | collective-permute-start | bytes 884744 | tf_op jit(solution)/shard_map/ppermute | solution.py:370
  50.2 1.4 %collective-permute-start.17 = (f32[192,384]{1,0:T(8,128)}, f32[192,384]{1,0:T(8,128)}, u32[]{:S(2)}, u32[]{:S(2)}) collective-permute-start(f32[192,384]{1,0:T(8,128)} %get-tuple-element.18), channel_id=1, source_target_pairs={{8,0},{9,1}} | collective-permute-start | bytes 884744 | tf_op jit(solution)/shard_map/ppermute | solution.py:370
  51.6 1.4 %collective-permute-start.16 = (f32[192,384]{1,0:T(8,128)}, f32[192,384]{1,0:T(8,128)}, u32[]{:S(2)}, u32[]{:S(2)}) collective-permute-start(f32[192,384]{1,0:T(8,128)} %collective-permute-done.15), channel_id=1, source_target_pairs={{16,24},{17,25}} | collective-permute-start | bytes 884744 | tf_op jit(solution)/shard_map/ppermute | solution.py:370
  53.7 1.4 %collective-permute-start.13 = (f32[192,384]{1,0:T(8,128)}, f32[192,384]{1,0:T(8,128)}, u32[]{:S(2)}, u32[]{:S(2)}) collective-permute-start(f32[192,384]{1,0:T(8,128)} %get-tuple-element.18), channel_id=1, source_target_pairs={{8,10},{9,13}} | collective-permute-start | bytes 884744 | tf_op jit(solution)/shard_map/ppermute | solution.py:370
  58.0 1.4 %collective-permute-start.11 = (f32[384,384]{1,0:T(8,128)S(1)}, f32[384,384]{1,0:T(8,128)S(1)}, u32[]{:S(2)}, u32[]{:S(2)}) collective-permute-start(f32[384,384]{1,0:T(8,128)S(1)} %broadcast_select_fusion.2), channel_id=1, source_target_pairs={{0,4},{16,20},{24,28},{2,6},{18,22},{26,30},{1,3},{17,19},{25,27},... | collective-permute-start | bytes 1769480 | tf_op jit(solution)/shard_map/ppermute | solution.py:370
  61.3 1.5 %collective-permute-start.6 = (f32[768,384]{1,0:T(8,128)S(1)}, f32[768,384]{1,0:T(8,128)S(1)}, u32[]{:S(2)}, u32[]{:S(2)}) collective-permute-start(f32[768,384]{1,0:T(8,128)S(1)} %copy-done.5), channel_id=1, source_target_pairs={{20,28},{21,29},{18,26},{27,19},{22,30},{31,23}} | collective-permute-start | bytes 3538952 | tf_op jit(solution)/shard_map/ppermute | solution.py:370
  64.5 1.3 collective-permute-start.19
  65.8 27.2 %collective-permute-done.11 = f32[384,384]{1,0:T(8,128)S(1)} collective-permute-done((f32[384,384]{1,0:T(8,128)S(1)}, f32[384,384]{1,0:T(8,128)S(1)}, u32[]{:S(2)}, u32[]{:S(2)}) %collective-permute-start.11) | collective-permute-done | bytes 589856 | tf_op jit(solution)/shard_map/ppermute | solution.py:370
  93.1 3.7 %collective-permute-start.12 = (f32[384,384]{1,0:T(8,128)S(1)}, f32[384,384]{1,0:T(8,128)}, u32[]{:S(2)}, u32[]{:S(2)}) collective-permute-start(f32[384,384]{1,0:T(8,128)S(1)} %broadcast_select_fusion.3.ng), channel_id=1, source_target_pairs={{0,1},{1,0},{2,3},{3,2},{4,5},{5,4},{6,7},{7,6},{8,9},{9,8},{10,11... | collective-permute-start | bytes 1769480 | tf_op jit(solution)/shard_map/ppermute | solution.py:370
  96.7 20.9 %collective-permute-done.19 = f32[192,384]{1,0:T(8,128)S(1)} collective-permute-done((f32[192,384]{1,0:T(8,128)S(1)}, f32[192,384]{1,0:T(8,128)S(1)}, u32[]{:S(2)}, u32[]{:S(2)}) %collective-permute-start.19) | collective-permute-done | bytes 294944 | tf_op jit(solution)/shard_map/ppermute | solution.py:370
  117.7 1.7 %collective-permute-start.20 = (f32[192,384]{1,0:T(8,128)S(1)}, f32[192,384]{1,0:T(8,128)S(1)}, u32[]{:S(2)}, u32[]{:S(2)}) collective-permute-start(f32[192,384]{1,0:T(8,128)S(1)} %select_select_fusion.1.s_mine), channel_id=1, source_target_pairs={{0,1},{1,0},{2,3},{3,2},{4,5},{5,4},{6,7},{7,6},{8,9},{9,8},{10,11... | collective-permute-start | bytes 884744 | tf_op jit(solution)/shard_map/ppermute | solution.py:370
  122.4 7.3 %finish.1 = f32[2304,128]{1,0:T(8,128)} custom-call(s32[5]{0:T(128)} %stack.74.flags, f32[768,384]{1,0:T(8,128)} %bitcast.17, f32[768,384]{1,0:T(8,128)} %copy-done.2, f32[768,384]{1,0:T(8,128)} %copy-done.4, f32[384,384]{1,0:T(8,128)} %copy-done.9, f32[768,384]{1,0:T(8,128)} %copy-done.3, f32[768,384]{1,0:T(8,128)} %copy-done.12, f32[768,384]{1,0:T(8,128)} %pack.1.packed, ...), custom_call_target="tpu_custom_call" | custom-call | tf_op jit(solution)/shard_map/finish/pallas_call | solution.py:344
  (65 shorter events, 18.3 us)
Async XLA Ops:
  1.2 9.4 %copy-start.6 = (f32[384,384]{1,0:T(8,128)}, f32[384,384]{1,0:T(8,128)S(1)}, u32[]{:S(2)}) copy-start(f32[384,384]{1,0:T(8,128)S(1)} %slice_bitcast_fusion.first) | copy-start | bytes 1769476
  1.2 2.4 %collective-permute-start = (f32[384,384]{1,0:T(8,128)S(1)}, f32[384,384]{1,0:T(8,128)S(1)}, u32[]{:S(2)}, u32[]{:S(2)}) collective-permute-start(f32[384,384]{1,0:T(8,128)S(1)} %slice_bitcast_fusion.first), channel_id=1, source_target_pairs={{0,1},{1,0},{2,3},{3,2},{4,5},{5,4},{6,7},{7,6},{8,9},{9,8},{10,11... | collective-permute-start | bytes 1769480 | tf_op jit(solution)/shard_map/ppermute | solution.py:370
  7.4 1.7 %collective-permute-start.1 = (f32[768,384]{1,0:T(8,128)}, f32[768,384]{1,0:T(8,128)}, u32[]{:S(2)}, u32[]{:S(2)}) collective-permute-start(f32[768,384]{1,0:T(8,128)} %get-tuple-element.12), channel_id=1, source_target_pairs={{0,2},{8,10},{16,18},{24,26},{1,5},{9,13},{17,21},{25,29}} | collective-permute-start | bytes 3538952 | tf_op jit(solution)/shard_map/ppermute | solution.py:370
  10.6 31.0 %collective-permute-start.2 = (f32[768,384]{1,0:T(8,128)S(1)}, f32[768,384]{1,0:T(8,128)}, u32[]{:S(2)}, u32[]{:S(2)}) collective-permute-start(f32[768,384]{1,0:T(8,128)S(1)} %broadcast_select_fusion), channel_id=1, source_target_pairs={{0,4},{8,12},{16,20},{24,28},{2,6},{10,14},{18,22},{26,30},{1,3},{... | collective-permute-start | bytes 3538952 | tf_op jit(solution)/shard_map/ppermute | solution.py:370
  12.8 3.7 %collective-permute-start.4 = (f32[384,384]{1,0:T(8,128)}, f32[384,384]{1,0:T(8,128)S(1)}, u32[]{:S(2)}, u32[]{:S(2)}) collective-permute-start(f32[384,384]{1,0:T(8,128)} %broadcast_select_fusion.4), channel_id=1, source_target_pairs={{0,8},{1,9},{2,10},{3,11},{4,12},{5,13},{6,14},{7,15},{10,2},{11,3... | collective-permute-start | bytes 1769480 | tf_op jit(solution)/shard_map/ppermute | solution.py:370
  13.5 5.2 %collective-permute-start.7 = (f32[384,384]{1,0:T(8,128)}, f32[384,384]{1,0:T(8,128)}, u32[]{:S(2)}, u32[]{:S(2)}) collective-permute-start(f32[384,384]{1,0:T(8,128)} %get-tuple-element.15), channel_id=1, source_target_pairs={{8,16},{9,17}} | collective-permute-start | bytes 1769480 | tf_op jit(solution)/shard_map/ppermute | solution.py:370
  15.0 30.1 %collective-permute-start.9 = (f32[384,384]{1,0:T(8,128)}, f32[384,384]{1,0:T(8,128)}, u32[]{:S(2)}, u32[]{:S(2)}) collective-permute-start(f32[384,384]{1,0:T(8,128)} %get-tuple-element.15), channel_id=1, source_target_pairs={{8,0},{9,1}} | collective-permute-start | bytes 1769480 | tf_op jit(solution)/shard_map/ppermute | solution.py:370
  18.0 35.7 %collective-permute-start.5 = (f32[768,384]{1,0:T(8,128)}, f32[768,384]{1,0:T(8,128)S(1)}, u32[]{:S(2)}, u32[]{:S(2)}) collective-permute-start(f32[768,384]{1,0:T(8,128)} %get-tuple-element.14), channel_id=1, source_target_pairs={{12,20},{13,21}} | collective-permute-start | bytes 3538952 | tf_op jit(solution)/shard_map/ppermute | solution.py:370
  18.8 26.4 %collective-permute-start.8 = (f32[384,384]{1,0:T(8,128)}, f32[384,384]{1,0:T(8,128)}, u32[]{:S(2)}, u32[]{:S(2)}) collective-permute-start(f32[384,384]{1,0:T(8,128)} %collective-permute-done.7), channel_id=1, source_target_pairs={{16,24},{17,25}} | collective-permute-start | bytes 1769480 | tf_op jit(solution)/shard_map/ppermute | solution.py:370
  43.0 4.3 %copy-start.2 = (f32[768,384]{1,0:T(8,128)}, f32[768,384]{1,0:T(8,128)S(1)}, u32[]{:S(2)}) copy-start(f32[768,384]{1,0:T(8,128)S(1)} %broadcast_select_fusion.1.lefts) | copy-start | bytes 3538948
  43.0 12.1 %collective-permute-start.3 = (f32[768,384]{1,0:T(8,128)S(1)}, f32[768,384]{1,0:T(8,128)S(1)}, u32[]{:S(2)}, u32[]{:S(2)}) collective-permute-start(f32[768,384]{1,0:T(8,128)S(1)} %broadcast_select_fusion.1.lefts), channel_id=1, source_target_pairs={{0,1},{1,0},{2,3},{3,2},{4,5},{5,4},{6,7},{7,6},{8,9},{9,8},{10,11... | collective-permute-start | bytes 3538952 | tf_op jit(solution)/shard_map/ppermute | solution.py:370
  47.3 9.5 %collective-permute-start.10 = (f32[384,384]{1,0:T(8,128)}, f32[384,384]{1,0:T(8,128)}, u32[]{:S(2)}, u32[]{:S(2)}) collective-permute-start(f32[384,384]{1,0:T(8,128)} %select_select_fusion), channel_id=1, source_target_pairs={{0,2},{16,18},{24,26},{1,5},{17,21},{25,29}} | collective-permute-start | bytes 1769480 | tf_op jit(solution)/shard_map/ppermute | solution.py:370
  48.8 2.8 %collective-permute-start.15 = (f32[192,384]{1,0:T(8,128)}, f32[192,384]{1,0:T(8,128)}, u32[]{:S(2)}, u32[]{:S(2)}) collective-permute-start(f32[192,384]{1,0:T(8,128)} %get-tuple-element.18), channel_id=1, source_target_pairs={{8,16},{9,17}} | collective-permute-start | bytes 884744 | tf_op jit(solution)/shard_map/ppermute | solution.py:370
  50.2 9.2 %collective-permute-start.17 = (f32[192,384]{1,0:T(8,128)}, f32[192,384]{1,0:T(8,128)}, u32[]{:S(2)}, u32[]{:S(2)}) collective-permute-start(f32[192,384]{1,0:T(8,128)} %get-tuple-element.18), channel_id=1, source_target_pairs={{8,0},{9,1}} | collective-permute-start | bytes 884744 | tf_op jit(solution)/shard_map/ppermute | solution.py:370
  51.6 7.8 %collective-permute-start.16 = (f32[192,384]{1,0:T(8,128)}, f32[192,384]{1,0:T(8,128)}, u32[]{:S(2)}, u32[]{:S(2)}) collective-permute-start(f32[192,384]{1,0:T(8,128)} %collective-permute-done.15), channel_id=1, source_target_pairs={{16,24},{17,25}} | collective-permute-start | bytes 884744 | tf_op jit(solution)/shard_map/ppermute | solution.py:370
  53.7 9.1 %collective-permute-start.13 = (f32[192,384]{1,0:T(8,128)}, f32[192,384]{1,0:T(8,128)}, u32[]{:S(2)}, u32[]{:S(2)}) collective-permute-start(f32[192,384]{1,0:T(8,128)} %get-tuple-element.18), channel_id=1, source_target_pairs={{8,10},{9,13}} | collective-permute-start | bytes 884744 | tf_op jit(solution)/shard_map/ppermute | solution.py:370
  58.0 35.0 %collective-permute-start.11 = (f32[384,384]{1,0:T(8,128)S(1)}, f32[384,384]{1,0:T(8,128)S(1)}, u32[]{:S(2)}, u32[]{:S(2)}) collective-permute-start(f32[384,384]{1,0:T(8,128)S(1)} %broadcast_select_fusion.2), channel_id=1, source_target_pairs={{0,4},{16,20},{24,28},{2,6},{18,22},{26,30},{1,3},{17,19},{25,27},... | collective-permute-start | bytes 1769480 | tf_op jit(solution)/shard_map/ppermute | solution.py:370
  60.6 3.9 %collective-permute-start.18 = (f32[192,384]{1,0:T(8,128)S(1)}, f32[192,384]{1,0:T(8,128)S(1)}, u32[]{:S(2)}, u32[]{:S(2)}) collective-permute-start(f32[192,384]{1,0:T(8,128)S(1)} %select_select_fusion.2), channel_id=1, source_target_pairs={{0,2},{16,18},{24,26},{1,5},{17,21},{25,29}} | collective-permute-start | bytes 884744 | tf_op jit(solution)/shard_map/ppermute | solution.py:370
  61.3 59.4 %collective-permute-start.6 = (f32[768,384]{1,0:T(8,128)S(1)}, f32[768,384]{1,0:T(8,128)S(1)}, u32[]{:S(2)}, u32[]{:S(2)}) collective-permute-start(f32[768,384]{1,0:T(8,128)S(1)} %copy-done.5), channel_id=1, source_target_pairs={{20,28},{21,29},{18,26},{27,19},{22,30},{31,23}} | collective-permute-start | bytes 3538952 | tf_op jit(solution)/shard_map/ppermute | solution.py:370
  63.8 33.0 %collective-permute-start.14 = (f32[192,384]{1,0:T(8,128)S(1)}, f32[192,384]{1,0:T(8,128)S(1)}, u32[]{:S(2)}, u32[]{:S(2)}) collective-permute-start(f32[192,384]{1,0:T(8,128)S(1)} %broadcast_select_fusion.6), channel_id=1, source_target_pairs={{8,12},{10,14},{9,11},{13,15}} | collective-permute-start | bytes 884744 | tf_op jit(solution)/shard_map/ppermute | solution.py:370
  64.5 53.1 %collective-permute-start.19 = (f32[192,384]{1,0:T(8,128)S(1)}, f32[192,384]{1,0:T(8,128)S(1)}, u32[]{:S(2)}, u32[]{:S(2)}) collective-permute-start(f32[192,384]{1,0:T(8,128)S(1)} %broadcast_select_fusion.5), channel_id=1, source_target_pairs={{0,4},{16,20},{24,28},{2,6},{18,22},{26,30},{1,3},{17,19},{25,27},... | collective-permute-start | bytes 884744 | tf_op jit(solution)/shard_map/ppermute | solution.py:370
  93.1 27.6 %copy-start.10 = (f32[384,384]{1,0:T(8,128)}, f32[384,384]{1,0:T(8,128)S(1)}, u32[]{:S(2)}) copy-start(f32[384,384]{1,0:T(8,128)S(1)} %broadcast_select_fusion.3.ng) | copy-start | bytes 1769476
  93.1 27.6 %collective-permute-start.12 = (f32[384,384]{1,0:T(8,128)S(1)}, f32[384,384]{1,0:T(8,128)}, u32[]{:S(2)}, u32[]{:S(2)}) collective-permute-start(f32[384,384]{1,0:T(8,128)S(1)} %broadcast_select_fusion.3.ng), channel_id=1, source_target_pairs={{0,1},{1,0},{2,3},{3,2},{4,5},{5,4},{6,7},{7,6},{8,9},{9,8},{10,11... | collective-permute-start | bytes 1769480 | tf_op jit(solution)/shard_map/ppermute | solution.py:370
  117.7 2.9 %collective-permute-start.20 = (f32[192,384]{1,0:T(8,128)S(1)}, f32[192,384]{1,0:T(8,128)S(1)}, u32[]{:S(2)}, u32[]{:S(2)}) collective-permute-start(f32[192,384]{1,0:T(8,128)S(1)} %select_select_fusion.1.s_mine), channel_id=1, source_target_pairs={{0,1},{1,0},{2,3},{3,2},{4,5},{5,4},{6,7},{7,6},{8,9},{9,8},{10,11... | collective-permute-start | bytes 884744 | tf_op jit(solution)/shard_map/ppermute | solution.py:370
  (11 other events, 20.2 us)
